TPU v7x, 32 devices: a whole 2x2x4 slice. The times are simulated.
32 devices in a mesh: shard: 4 (over x, core), replica: 8 (over z, y).
Axes of the slice: x: 2, y: 2, z: 4, core: 2. Of those that a mesh axis runs over, the one named last changes fastest.
Arguments:
- tokens: bfloat16 [16384, 768], P(('shard', 'replica')), may hold values from -6 to 6
- cotangent: bfloat16 [16384, 768], P(('shard', 'replica')), may hold values from -6 to 6
- lengths: int32 [32], replicated, may hold values from 16 to 512, as said below
- assignment: int32 [32], replicated, may hold values from 0 to 31, as said below
- positions: int32 [16384], P(('shard', 'replica')), may hold values from 0 to 2047, as said below
- attention_gain: bfloat16 [768], P('shard'), may hold values from 0.25 to 2.5
- query_weight: bfloat16 [768, 768], P('shard'), may hold values from -0.21875 to 0.21875
- key_weight: bfloat16 [768, 768], P('shard'), may hold values from -0.21875 to 0.21875
- value_weight: bfloat16 [768, 768], P('shard'), may hold values from -0.21875 to 0.21875
- out_weight: bfloat16 [768, 768], P('shard'), may hold values from -1.25 to 1.25
- feedforward_gain: bfloat16 [768], P('shard'), may hold values from 0.25 to 2.5
- gate_weight: bfloat16 [768, 3072], P('shard'), may hold values from -0.21875 to 0.21875
- up_weight: bfloat16 [768, 3072], P('shard'), may hold values from -0.21875 to 0.21875
- down_weight: bfloat16 [3072, 768], P('shard'), may hold values from -0.21875 to 0.21875
Outputs:
- output: bfloat16 [16384, 768], P(('shard', 'replica'))
- input_grad: float32 [16384, 768], P(('shard', 'replica'))
- attention_gain_grad: float32 [768], P('shard')
- query_grad: float32 [768, 768], P('shard')
- key_grad: float32 [768, 768], P('shard')
- value_grad: float32 [768, 768], P('shard')
- out_grad: float32 [768, 768], P('shard')
- feedforward_gain_grad: float32 [768], P('shard')
- gate_grad: float32 [768, 3072], P('shard')
- up_grad: float32 [768, 3072], P('shard')
- down_grad: float32 [3072, 768], P('shard')
Inputs may be any that keep to these rules, and one draw needn't show every extreme that they name: `lengths`: each block holds exactly 1 sequence, 16 to 512 rows long; in some block it is exactly 512 rows long. `assignment`: every block index is named by exactly 1 sequence. Within a sequence, positions rise by one from row to row from a start between 0 and 2048 minus the sequence's length; empty rows hold 0.
All inputs are finite; a program needn't handle non-finite values.
Results may differ from a plain program's by a relative error of at most 0.023.
Values may be sent and summed in bfloat16 or wider, within the bound.
A program may use at most 192 MiB of HBM per device.

v0:
```python
import math
import jax
import jax.numpy as jnp
from jax import lax
from jax.sharding import PartitionSpec as P

HEADS = 12
HDIM = 64
EPSILON = 1e-05
ROPE_BASE = 10000.0


def rms_scale(values):
    return lax.rsqrt(jnp.mean(values * values, axis=-1, keepdims=True) + EPSILON)


def rotation(positions, head_size):
    half_size = head_size // 2
    steps_range = jnp.arange(half_size, dtype=jnp.float32)
    frequency = jnp.exp(steps_range * (-2.0 * math.log(ROPE_BASE) / head_size))
    angles = positions.astype(jnp.float32)[:, None] * frequency[None, :]
    return (jnp.cos(angles), jnp.sin(angles))


def rotate(values, cosine_table, sine_table):
    half_size = cosine_table.shape[1]
    shaped = values.reshape(values.shape[0], -1, 2 * half_size)
    first_half = shaped[..., :half_size]
    second_half = shaped[..., half_size:]
    cos_rows = cosine_table[:, None, :]
    sin_rows = sine_table[:, None, :]
    turned = jnp.concatenate(
        [
            first_half * cos_rows - second_half * sin_rows,
            second_half * cos_rows + first_half * sin_rows,
        ],
        axis=-1,
    )
    return turned.reshape(values.shape)


def rotate_back(values, cosine_table, sine_table):
    half_size = cosine_table.shape[1]
    shaped = values.reshape(values.shape[0], -1, 2 * half_size)
    first_half = shaped[..., :half_size]
    second_half = shaped[..., half_size:]
    cos_rows = cosine_table[:, None, :]
    sin_rows = sine_table[:, None, :]
    turned = jnp.concatenate(
        [
            first_half * cos_rows + second_half * sin_rows,
            second_half * cos_rows - first_half * sin_rows,
        ],
        axis=-1,
    )
    return turned.reshape(values.shape)


def sequence_mask(lengths, assignment, device, slot_count):
    owned_lengths = jnp.where(assignment == device, lengths, 0)
    seq_ends = jnp.cumsum(owned_lengths)
    slot_ids = jnp.arange(slot_count, dtype=jnp.int32)
    labels = jnp.sum((seq_ends[None, :] <= slot_ids[:, None]).astype(jnp.int32), axis=1)
    allowed = (labels[:, None] == labels[None, :]) & (slot_ids[None, :] <= slot_ids[:, None])
    valid_rows = (slot_ids < seq_ends[-1]).astype(jnp.float32)[:, None]
    return (allowed, valid_rows)


def by_group(values, groups):
    return jnp.moveaxis(values.reshape(values.shape[0], groups, -1, HDIM), 1, 0)


def from_group(values):
    moved = jnp.moveaxis(values, 0, 1)
    return moved.reshape(moved.shape[0], -1)


def norm_back(grad_normed, values, scale_rows, gain):
    scaled_grad = gain * grad_normed
    gain_grad = jnp.sum(grad_normed * values * scale_rows, axis=0)
    grad_values = scale_rows * scaled_grad - values * scale_rows**3 * jnp.mean(
        scaled_grad * values, axis=-1, keepdims=True
    )
    return (gain_grad, grad_values)


def per_device(
    tokens,
    cotangent,
    lengths,
    assignment,
    positions,
    attention_gain,
    query_weight,
    key_weight,
    value_weight,
    out_weight,
    feedforward_gain,
    gate_weight,
    up_weight,
    down_weight,
):
    slot_count = tokens.shape[0]
    heads_per = math.gcd(HEADS, 4)
    groups = HEADS // heads_per
    inv_root = 1.0 / math.sqrt(HDIM)
    device = lax.axis_index("shard") * lax.axis_size("replica") + lax.axis_index("replica")
    allowed, valid_rows = sequence_mask(lengths, assignment, device, slot_count)
    cosine_table, sine_table = rotation(positions, HDIM)
    gain_one, w_query, w_key, w_value, w_out = (
        lax.all_gather(attention_gain, "shard", axis=0, tiled=True),
        lax.all_gather(query_weight, "shard", axis=0, tiled=True),
        lax.all_gather(key_weight, "shard", axis=0, tiled=True),
        lax.all_gather(value_weight, "shard", axis=0, tiled=True),
        lax.all_gather(out_weight, "shard", axis=0, tiled=True),
    )
    values = tokens.astype(jnp.float32)
    scale_one = rms_scale(values)
    normed = (values * scale_one * gain_one.astype(jnp.float32)).astype(jnp.bfloat16)
    query_lin = jnp.dot(normed, w_query, preferred_element_type=jnp.float32)
    key_lin = jnp.dot(normed, w_key, preferred_element_type=jnp.float32)
    value_low = jnp.dot(normed, w_value, preferred_element_type=jnp.float32).astype(jnp.bfloat16)
    query_rot = rotate(query_lin, cosine_table, sine_table).astype(jnp.bfloat16)
    key_rot = rotate(key_lin, cosine_table, sine_table).astype(jnp.bfloat16)
    query_groups = by_group(query_rot, groups)
    key_groups = by_group(key_rot, groups)
    value_groups = by_group(value_low, groups)

    def attend(group_in):
        query_part, key_part, value_part = group_in
        scores = (
            jnp.einsum("qhd,khd->hqk", query_part, key_part, preferred_element_type=jnp.float32)
            * inv_root
        )
        scores = jnp.where(allowed[None], scores, -jnp.inf)
        row_peak = jnp.max(scores, axis=-1, keepdims=True)
        exponent = jnp.exp(scores - row_peak)
        row_total = jnp.sum(exponent, axis=-1, keepdims=True)
        probability = (exponent / row_total).astype(jnp.bfloat16)
        mixed_values = jnp.einsum(
            "hqk,khd->qhd", probability, value_part, preferred_element_type=jnp.float32
        )
        return (mixed_values, row_peak[..., 0] + jnp.log(row_total[..., 0]))

    mixed_groups, log_totals = lax.map(attend, (query_groups, key_groups, value_groups))
    attended = from_group(mixed_groups).astype(jnp.bfloat16)
    hidden_one = values + jnp.dot(attended, w_out, preferred_element_type=jnp.float32)
    gain_two, w_gate, w_up, w_down = (
        lax.all_gather(feedforward_gain, "shard", axis=0, tiled=True),
        lax.all_gather(gate_weight, "shard", axis=0, tiled=True),
        lax.all_gather(up_weight, "shard", axis=0, tiled=True),
        lax.all_gather(down_weight, "shard", axis=0, tiled=True),
    )
    scale_two = rms_scale(hidden_one)
    normed_two = (hidden_one * scale_two * gain_two.astype(jnp.float32)).astype(jnp.bfloat16)
    gate = jnp.dot(normed_two, w_gate, preferred_element_type=jnp.float32)
    upward = jnp.dot(normed_two, w_up, preferred_element_type=jnp.float32)
    sigmoid_gate = jax.nn.sigmoid(gate)
    activated = gate * sigmoid_gate
    hidden = (activated * upward).astype(jnp.bfloat16)
    branch_two = jnp.dot(hidden, w_down, preferred_element_type=jnp.float32)
    output = ((hidden_one + branch_two) * valid_rows).astype(jnp.bfloat16)
    gain_two, w_gate, w_up, w_down = (
        lax.all_gather(feedforward_gain, "shard", axis=0, tiled=True),
        lax.all_gather(gate_weight, "shard", axis=0, tiled=True),
        lax.all_gather(up_weight, "shard", axis=0, tiled=True),
        lax.all_gather(down_weight, "shard", axis=0, tiled=True),
    )
    grad_out = cotangent.astype(jnp.float32) * valid_rows
    grad_branch_two = grad_out.astype(jnp.bfloat16)
    grad_down = jnp.einsum("nf,nd->fd", hidden, grad_branch_two, preferred_element_type=jnp.float32)
    grad_hidden = jnp.einsum(
        "nd,fd->nf", grad_branch_two, w_down, preferred_element_type=jnp.float32
    )
    grad_gate = (grad_hidden * upward * sigmoid_gate * (1.0 + gate * (1.0 - sigmoid_gate))).astype(
        jnp.bfloat16
    )
    grad_up = (grad_hidden * activated).astype(jnp.bfloat16)
    grad_gate_weight = jnp.einsum(
        "nd,nf->df", normed_two, grad_gate, preferred_element_type=jnp.float32
    )
    grad_up_weight = jnp.einsum(
        "nd,nf->df", normed_two, grad_up, preferred_element_type=jnp.float32
    )
    grad_normed_two = jnp.einsum(
        "nf,df->nd", grad_gate, w_gate, preferred_element_type=jnp.float32
    ) + jnp.einsum("nf,df->nd", grad_up, w_up, preferred_element_type=jnp.float32)
    grad_gain_two, grad_norm_two = norm_back(
        grad_normed_two, hidden_one, scale_two, gain_two.astype(jnp.float32)
    )
    grad_hidden_one = grad_out + grad_norm_two
    ffn_terms = (grad_gain_two, grad_gate_weight, grad_up_weight, grad_down)
    ffn_shares = (
        lax.psum_scatter(
            ffn_terms[0].astype(jnp.bfloat16), "shard", scatter_dimension=0, tiled=True
        ).astype(jnp.float32),
        lax.psum_scatter(
            ffn_terms[1].astype(jnp.bfloat16), "shard", scatter_dimension=0, tiled=True
        ).astype(jnp.float32),
        lax.psum_scatter(
            ffn_terms[2].astype(jnp.bfloat16), "shard", scatter_dimension=0, tiled=True
        ).astype(jnp.float32),
        lax.psum_scatter(
            ffn_terms[3].astype(jnp.bfloat16), "shard", scatter_dimension=0, tiled=True
        ).astype(jnp.float32),
    )
    ffn_sums = (
        lax.psum(ffn_shares[0].astype(jnp.bfloat16), "replica").astype(jnp.float32),
        lax.psum(ffn_shares[1].astype(jnp.bfloat16), "replica").astype(jnp.float32),
        lax.psum(ffn_shares[2].astype(jnp.bfloat16), "replica").astype(jnp.float32),
        lax.psum(ffn_shares[3].astype(jnp.bfloat16), "replica").astype(jnp.float32),
    )
    gain_one, w_query, w_key, w_value, w_out = (
        lax.all_gather(attention_gain, "shard", axis=0, tiled=True),
        lax.all_gather(query_weight, "shard", axis=0, tiled=True),
        lax.all_gather(key_weight, "shard", axis=0, tiled=True),
        lax.all_gather(value_weight, "shard", axis=0, tiled=True),
        lax.all_gather(out_weight, "shard", axis=0, tiled=True),
    )
    grad_branch_one = grad_hidden_one.astype(jnp.bfloat16)
    grad_out_weight = jnp.einsum(
        "nd,ne->de", attended, grad_branch_one, preferred_element_type=jnp.float32
    )
    grad_attended = jnp.einsum(
        "ne,de->nd", grad_branch_one, w_out, preferred_element_type=jnp.float32
    ).astype(jnp.bfloat16)
    grad_groups = by_group(grad_attended, groups)

    def attend_back(group_in):
        query_part, key_part, value_part, grad_part, log_total = group_in
        scores = (
            jnp.einsum("qhd,khd->hqk", query_part, key_part, preferred_element_type=jnp.float32)
            * inv_root
        )
        scores = jnp.where(allowed[None], scores, -jnp.inf)
        probability = jnp.exp(scores - log_total[..., None])
        probability_low = probability.astype(jnp.bfloat16)
        grad_value = jnp.einsum(
            "hqk,qhd->khd", probability_low, grad_part, preferred_element_type=jnp.float32
        )
        grad_probability = jnp.einsum(
            "qhd,khd->hqk", grad_part, value_part, preferred_element_type=jnp.float32
        )
        row_dot = jnp.sum(probability * grad_probability, axis=-1, keepdims=True)
        grad_scores = (probability * (grad_probability - row_dot)).astype(jnp.bfloat16)
        grad_query = (
            jnp.einsum("hqk,khd->qhd", grad_scores, key_part, preferred_element_type=jnp.float32)
            * inv_root
        )
        grad_key = (
            jnp.einsum("hqk,qhd->khd", grad_scores, query_part, preferred_element_type=jnp.float32)
            * inv_root
        )
        return (grad_query, grad_key, grad_value)

    grad_query_groups, grad_key_groups, grad_value_groups = lax.map(
        attend_back, (query_groups, key_groups, value_groups, grad_groups, log_totals)
    )
    grad_query_lin = rotate_back(from_group(grad_query_groups), cosine_table, sine_table).astype(
        jnp.bfloat16
    )
    grad_key_lin = rotate_back(from_group(grad_key_groups), cosine_table, sine_table).astype(
        jnp.bfloat16
    )
    grad_value_lin = from_group(grad_value_groups).astype(jnp.bfloat16)
    grad_query_weight = jnp.einsum(
        "nd,ne->de", normed, grad_query_lin, preferred_element_type=jnp.float32
    )
    grad_key_weight = jnp.einsum(
        "nd,ne->de", normed, grad_key_lin, preferred_element_type=jnp.float32
    )
    grad_value_weight = jnp.einsum(
        "nd,ne->de", normed, grad_value_lin, preferred_element_type=jnp.float32
    )
    grad_normed = jnp.einsum(
        "ne,de->nd", grad_query_lin, w_query, preferred_element_type=jnp.float32
    )
    grad_normed = grad_normed + jnp.einsum(
        "ne,de->nd", grad_key_lin, w_key, preferred_element_type=jnp.float32
    )
    grad_normed = grad_normed + jnp.einsum(
        "ne,de->nd", grad_value_lin, w_value, preferred_element_type=jnp.float32
    )
    grad_gain_one, grad_norm_one = norm_back(
        grad_normed, values, scale_one, gain_one.astype(jnp.float32)
    )
    input_grad = grad_hidden_one + grad_norm_one
    attn_terms = (
        grad_gain_one,
        grad_query_weight,
        grad_key_weight,
        grad_value_weight,
        grad_out_weight,
    )
    attn_shares = (
        lax.psum_scatter(
            attn_terms[0].astype(jnp.bfloat16), "shard", scatter_dimension=0, tiled=True
        ).astype(jnp.float32),
        lax.psum_scatter(
            attn_terms[1].astype(jnp.bfloat16), "shard", scatter_dimension=0, tiled=True
        ).astype(jnp.float32),
        lax.psum_scatter(
            attn_terms[2].astype(jnp.bfloat16), "shard", scatter_dimension=0, tiled=True
        ).astype(jnp.float32),
        lax.psum_scatter(
            attn_terms[3].astype(jnp.bfloat16), "shard", scatter_dimension=0, tiled=True
        ).astype(jnp.float32),
        lax.psum_scatter(
            attn_terms[4].astype(jnp.bfloat16), "shard", scatter_dimension=0, tiled=True
        ).astype(jnp.float32),
    )
    attn_sums = (
        lax.psum(attn_shares[0].astype(jnp.bfloat16), "replica").astype(jnp.float32),
        lax.psum(attn_shares[1].astype(jnp.bfloat16), "replica").astype(jnp.float32),
        lax.psum(attn_shares[2].astype(jnp.bfloat16), "replica").astype(jnp.float32),
        lax.psum(attn_shares[3].astype(jnp.bfloat16), "replica").astype(jnp.float32),
        lax.psum(attn_shares[4].astype(jnp.bfloat16), "replica").astype(jnp.float32),
    )
    return (
        output,
        input_grad,
        attn_sums[0],
        attn_sums[1],
        attn_sums[2],
        attn_sums[3],
        attn_sums[4],
        ffn_sums[0],
        ffn_sums[1],
        ffn_sums[2],
        ffn_sums[3],
    )


def solution(mesh):
    return jax.shard_map(
        per_device,
        mesh=mesh,
        in_specs=(
            P(("shard", "replica"), None),
            P(("shard", "replica"), None),
            P(),
            P(),
            P(("shard", "replica")),
            P("shard"),
            P("shard", None),
            P("shard", None),
            P("shard", None),
            P("shard", None),
            P("shard"),
            P("shard", None),
            P("shard", None),
            P("shard", None),
        ),
        out_specs=(
            P(("shard", "replica"), None),
            P(("shard", "replica"), None),
            P("shard"),
            P("shard", None),
            P("shard", None),
            P("shard", None),
            P("shard", None),
            P("shard"),
            P("shard", None),
            P("shard", None),
            P("shard", None),
        ),
        check_vma=False,
    )
```

profile of v0, /device:TPU:0, one launch (start us, length us, event | category | flops | bytes accessed | tf_op | source)
XLA Modules:
  0.0 718.3 jit_solution(7855634631792464619)
XLA Ops:
  15.5 8.7 %all-reduce.7 = (bf16[768]{0:T(1024)(128)(2,1)S(1)}, bf16[768]{0:T(1024)(128)(2,1)S(1)}) all-reduce(bf16[768]{0:T(1024)(128)(2,1)S(1)} %dynamic-update-slice, bf16[768]{0:T(1024)(128)(2,1)S(1)} %dynamic-update-slice.1), channel_id=1, replica_groups=mesh['shard'=4,'replica'=8] {'shard'}, use_global_device_ids=true, to_apply=%add | all-reduce | flops 1536 | bytes 6144
  25.1 2.1 copy.79
  28.2 1.6 all-gather.8.cloned.1.call-done
  29.8 2.1 convolution_convert_fusion.8
  31.9 1.2 copy.60
  33.0 15.8 %all-gather.10.cloned.1.call-done = bf16[768,768]{1,0:T(8,128)(2,1)} async-done(((bf16[192,768]{1,0:T(8,128)(2,1)}), bf16[768,768]{1,0:T(8,128)(2,1)}) %all-gather.10.cloned.1.call-update) | async-done | bytes 1179664 | tf_op jit(solution)/shard_map/all_gather | solution.py:112
  48.9 2.2 fusion.82
  51.1 16.9 %all-gather.12.cloned.1.call-done = bf16[768,768]{1,0:T(8,128)(2,1)} async-done(((bf16[192,768]{1,0:T(8,128)(2,1)}), bf16[768,768]{1,0:T(8,128)(2,1)}) %all-gather.12.cloned.1.call-update) | async-done | bytes 1179664 | tf_op jit(solution)/shard_map/all_gather | solution.py:113
  67.9 2.2 fusion.80
  70.8 15.3 %while.30 = (s32[]{:T(128)}, bf16[3,512,4,64]{1,3,2,0:T(8,128)(2,1)}, f32[3,4,512]{2,1,0:T(4,128)S(1)}, bf16[3,512,4,64]{1,3,2,0:T(8,128)(2,1)}, bf16[3,512,4,64...) while((s32[]{:T(128)}, ...), condition=%wide.region_6.7_spmd.clone.clone, body=%wide.region_3.6_spmd.clone.sunk.clone | while | flops 281802752 | bytes 15011921 | solution.py:145
  72.8 3.0 fusion.166
  77.9 3.0 fusion.166
  83.0 3.0 fusion.166
  86.8 2.4 multiply_reduce_fusion.3
  90.6 35.1 %all-gather.16.cloned.1.call-done = bf16[768,3072]{1,0:T(8,128)(2,1)} async-done(((bf16[192,3072]{1,0:T(8,128)(2,1)}), bf16[768,3072]{1,0:T(8,128)(2,1)}) %all-gather.16.cloned.1.call-update) | async-done | bytes 4718608 | tf_op jit(solution)/shard_map/all_gather | solution.py:150
  125.7 6.8 fusion.87
  132.5 32.1 %all-gather.18.cloned.1.call-done = bf16[768,3072]{1,0:T(8,128)(2,1)} async-done(((bf16[192,3072]{1,0:T(8,128)(2,1)}), bf16[768,3072]{1,0:T(8,128)(2,1)}) %all-gather.18.cloned.1.call-update) | async-done | bytes 4718608 | tf_op jit(solution)/shard_map/all_gather | solution.py:151
  164.6 6.8 fusion.88
  171.4 32.2 %all-gather.20.cloned.1.call-done = bf16[3072,768]{1,0:T(8,128)(2,1)} async-done(((bf16[768,768]{1,0:T(8,128)(2,1)}), bf16[3072,768]{1,0:T(8,128)(2,1)}) %all-gather.20.cloned.1.call-update) | async-done | bytes 4718608 | tf_op jit(solution)/shard_map/all_gather | solution.py:152
  203.6 10.4 %multiply_convert_fusion.1 = (bf16[512,3072]{1,0:T(8,128)(2,1)S(1)}, bf16[512,3072]{1,0:T(8,128)(2,1)S(1)}, bf16[512,3072]{1,0:T(8,128)(2,1)}) fusion(f32[512,3072]{1,0:T(8,128)} %fusion.87, f32[512,3072]{1,0:T(8,128)} %fusion.88, bf16[3072,768]{1,0:T(8,128)(2,1)} %all-gather.20.cloned.1.call-done, bf16[512,768]{1,0:T(8,128)(2,1)S(1)} %copy-done.12, ...), kind=kOutput, calls=%fused_computation.64 | convolution fusion | flops 2440691712 | bytes 27527168 | tf_op jit(solution)/shard_map/nd,fd->nf/dot_general | solution.py:172
  214.0 7.3 %fusion.89 = f32[512,768]{1,0:T(8,128)S(1)} fusion(bf16[512,3072]{1,0:T(8,128)(2,1)S(1)} %get-tuple-element.204, bf16[768,3072]{1,0:T(8,128)(2,1)} %all-gather.16.cloned.1.call-done), kind=kOutput, calls=%fused_computation.139 | convolution fusion | flops 2415919104 | bytes 9437184 | tf_op jit(solution)/shard_map/nf,df->nd/dot_general | solution.py:185
  221.4 3.0 multiply_reduce_fusion.1
  225.6 1.7 convolution_convert_fusion.7
  227.3 2.3 copy.64
  229.7 28.9 %while.31 = (s32[]{:T(128)}, f32[3,512,4,64]{1,3,2,0:T(8,128)}, f32[3,512,4,64]{1,3,2,0:T(8,128)}, bf16[3,512,4,64]{1,3,2,0:T(8,128)(2,1)}, bf16[3,512,4,64]{1,3...) while((s32[]{:T(128)}, f32[3,512,4,64]{1,3,2,0:T(8,128)}, ...), condition=%wide.region_11.12_spmd.clone.clone, body=%wide.region_9.11_spmd.clone.sunk.clone | while | flops 687863808 | bytes 39124100 | solution.py:256
  231.0 2.5 multiply_reduce_fusion.6
  233.4 1.3 multiply_convert_fusion.8
  234.7 1.6 fusion.178
  236.2 1.3 fusion.177
  237.5 1.9 fusion.179
  240.6 2.4 multiply_reduce_fusion.6
  243.0 1.3 multiply_convert_fusion.8
  244.3 1.6 fusion.178
  245.8 1.3 fusion.177
  247.1 1.9 fusion.179
  250.2 2.4 multiply_reduce_fusion.6
  252.6 1.3 multiply_convert_fusion.8
  253.9 1.6 fusion.178
  255.4 1.3 fusion.177
  256.7 1.9 fusion.179
  258.6 2.4 add_convert_fusion
  262.4 2.0 convolution_convert_fusion.5
  265.4 2.0 convolution_convert_fusion.6
  267.5 2.9 convolution_convert_fusion.3
  270.5 3.3 convolution_convert_fusion.4
  273.8 6.2 convolution_convert_fusion.2
  280.1 6.3 convolution_convert_fusion.1
  287.6 6.8 convolution_convert_fusion
  294.5 24.4 %reduce-scatter.8.cloned.1.call-done = bf16[192,768]{1,0:T(8,128)(2,1)} async-done(((bf16[768,768]{1,0:T(8,128)(2,1)}), bf16[192,768]{1,0:T(8,128)(2,1)}) %reduce-scatter.8.cloned.1.call-update) | async-done | bytes 294928 | tf_op jit(solution)/shard_map/reduce_scatter | solution.py:299
  319.0 28.1 %reduce-scatter.14.cloned.1.call-done = bf16[192,768]{1,0:T(8,128)(2,1)} async-done(((bf16[768,768]{1,0:T(8,128)(2,1)}), bf16[192,768]{1,0:T(8,128)(2,1)}) %reduce-scatter.14.cloned.1.call-update) | async-done | bytes 294928 | tf_op jit(solution)/shard_map/reduce_scatter | solution.py:308
  347.0 28.8 %reduce-scatter.12.cloned.1.call-done = bf16[192,768]{1,0:T(8,128)(2,1)} async-done(((bf16[768,768]{1,0:T(8,128)(2,1)}), bf16[192,768]{1,0:T(8,128)(2,1)}) %reduce-scatter.12.cloned.1.call-update) | async-done | bytes 294928 | tf_op jit(solution)/shard_map/reduce_scatter | solution.py:305
  375.8 50.4 %reduce-scatter.16.cloned.1.call-done = bf16[192,3072]{1,0:T(8,128)(2,1)} async-done(((bf16[768,3072]{1,0:T(8,128)(2,1)}), bf16[192,3072]{1,0:T(8,128)(2,1)}) %reduce-scatter.16.cloned.1.call-update) | async-done | bytes 1179664 | tf_op jit(solution)/shard_map/reduce_scatter | solution.py:197
  426.2 50.5 %reduce-scatter.18.cloned.1.call-done = bf16[192,3072]{1,0:T(8,128)(2,1)} async-done(((bf16[768,3072]{1,0:T(8,128)(2,1)}), bf16[192,3072]{1,0:T(8,128)(2,1)}) %reduce-scatter.18.cloned.1.call-update) | async-done | bytes 1179664 | tf_op jit(solution)/shard_map/reduce_scatter | solution.py:200
  476.7 50.4 %reduce-scatter.20.cloned.1.call-done = bf16[768,768]{1,0:T(8,128)(2,1)} async-done(((bf16[3072,768]{1,0:T(8,128)(2,1)}), bf16[768,768]{1,0:T(8,128)(2,1)}) %reduce-scatter.20.cloned.1.call-update) | async-done | bytes 1179664 | tf_op jit(solution)/shard_map/reduce_scatter | solution.py:203
  528.2 2.2 fusion.91
  531.8 3.5 fusion.68
  535.2 5.7 all-reduce.6
  541.1 23.0 %all-reduce.4 = (bf16[192]{0:T(256)(128)(2,1)S(1)}, bf16[192]{0:T(256)(128)(2,1)S(1)}) all-reduce(bf16[192]{0:T(256)(128)(2,1)S(1)} %dynamic-slice.3, bf16[192]{0:T(256)(128)(2,1)S(1)} %dynamic-slice.5), channel_id=1, replica_groups=mesh['shard'=4,'replica'=8] {'replica'}, use_global_device_ids=true, to_apply=%region_15.16 | all-reduce | flops 384 | bytes 1536 | tf_op jit(solution)/shard_map/psum | solution.py:313
  565.2 3.1 fusion.65
  568.4 5.8 multiply_convert_fusion.4
  574.2 127.6 %all-reduce.10.cloned.1.call-done = (bf16[192,768]{1,0:T(8,128)(2,1)}, bf16[192,768]{1,0:T(8,128)(2,1)}, bf16[192,768]{1,0:T(8,128)(2,1)}, bf16[192,768]{1,0:T(8...) async-done(((bf16[192,768]{1,0:T(8,128)(2,1)}, bf16[192,768]{1,0:T(8,128)(2,1)}, bf16[192,768]{1,0:T(8,128)(2,1)}, ...) | async-done | bytes 4718608 | tf_op jit(solution)/shard_map/psum | solution.py:314
  701.8 3.0 convert_element_type.214
  704.8 1.7 convert_element_type.216
  706.5 1.6 convert_element_type.218
  (168 shorter events, 33.1 us)
Async XLA Ops:
  7.2 22.6 %all-gather.8.cloned.1.call-start = ((), (), s32[]{:S(2)}) async-start(), calls=%async_computation.7 | async-start | bytes 1474560 | tf_op jit(solution)/shard_map/all_gather | solution.py:114
  7.9 41.0 %all-gather.10.cloned.1.call-start = ((), (), s32[]{:S(2)}) async-start(), calls=%async_computation.8 | async-start | bytes 1474560 | tf_op jit(solution)/shard_map/all_gather | solution.py:112
  8.7 59.3 %all-gather.12.cloned.1.call-start = ((), (), s32[]{:S(2)}) async-start(), calls=%async_computation.9 | async-start | bytes 1474560 | tf_op jit(solution)/shard_map/all_gather | solution.py:113
  9.4 77.4 %all-gather.14.cloned.1.call-start = ((), (), s32[]{:S(2)}) async-start(), calls=%async_computation.10 | async-start | bytes 1474560 | tf_op jit(solution)/shard_map/all_gather | solution.py:115
  10.0 115.7 %all-gather.16.cloned.1.call-start = ((), (), s32[]{:S(2)}) async-start(), calls=%async_computation.11 | async-start | bytes 5898240 | tf_op jit(solution)/shard_map/all_gather | solution.py:150
  10.6 2.4 copy-start.26
  10.6 2.4 copy-start.27
  10.6 3.2 copy-start.24
  10.6 4.4 copy-start.30
  10.6 4.7 copy-start.31
  10.6 13.6 %copy-start = (bf16[512,768]{1,0:T(8,128)(2,1)S(1)}, bf16[512,768]{1,0:T(8,128)(2,1)}, u32[]{:S(2)}) copy-start(bf16[512,768]{1,0:T(8,128)(2,1)} %param.18) | copy-start | bytes 2359300
  10.6 153.9 %all-gather.18.cloned.1.call-start = ((), (), s32[]{:S(2)}) async-start(), calls=%async_computation.12 | async-start | bytes 5898240 | tf_op jit(solution)/shard_map/all_gather | solution.py:151
  11.2 13.8 %copy-start.25 = (s32[512]{0:T(512)S(1)}, s32[512]{0:T(512)}, u32[]{:S(2)}) copy-start(s32[512]{0:T(512)} %param.22) | copy-start | bytes 6148
  11.2 192.4 %all-gather.20.cloned.1.call-start = ((), (), s32[]{:S(2)}) async-start(), calls=%async_computation.13 | async-start | bytes 5898240 | tf_op jit(solution)/shard_map/all_gather | solution.py:152
  12.0 282.6 %reduce-scatter.10.cloned.1.call-start = ((), (), s32[]{:S(2)}) async-start(), calls=%async_computation.15 | async-start | bytes 1474560 | tf_op jit(solution)/shard_map/reduce_scatter | solution.py:302
  89.2 1.1 copy-start.4
  90.6 74.0 %copy-start.2 = (bf16[512,768]{1,0:T(8,128)(2,1)}, bf16[512,768]{1,0:T(8,128)(2,1)S(1)}, u32[]{:S(2)}) copy-start(bf16[512,768]{1,0:T(8,128)(2,1)S(1)} %multiply_convert_fusion.5) | copy-start | bytes 2359300
  132.5 71.1 %copy-start.12 = (bf16[512,768]{1,0:T(8,128)(2,1)S(1)}, bf16[512,768]{1,0:T(8,128)(2,1)}, u32[]{:S(2)}) copy-start(bf16[512,768]{1,0:T(8,128)(2,1)} %param.19) | copy-start | bytes 2359300
  214.0 7.3 %copy-start.33 = (bf16[512,3072]{1,0:T(8,128)(2,1)}, bf16[512,3072]{1,0:T(8,128)(2,1)S(1)}, u32[]{:S(2)}) copy-start(bf16[512,3072]{1,0:T(8,128)(2,1)S(1)} %get-tuple-element.204) | copy-start | bytes 9437188
  214.0 7.3 %copy-start.32 = (bf16[512,3072]{1,0:T(8,128)(2,1)}, bf16[512,3072]{1,0:T(8,128)(2,1)S(1)}, u32[]{:S(2)}) copy-start(bf16[512,3072]{1,0:T(8,128)(2,1)S(1)} %get-tuple-element.203) | copy-start | bytes 9437188
  214.0 7.3 %copy-start.5 = (f32[512,768]{1,0:T(8,128)S(1)}, f32[512,768]{1,0:T(8,128)}, u32[]{:S(2)}) copy-start(f32[512,768]{1,0:T(8,128)} %copy-done.4) | copy-start | bytes 4718596
  214.0 7.3 %copy-start.8 = (bf16[768,3072]{1,0:T(8,128)(2,1)S(1)}, bf16[768,3072]{1,0:T(8,128)(2,1)}, u32[]{:S(2)}) copy-start(bf16[768,3072]{1,0:T(8,128)(2,1)} %all-gather.18.cloned.1.call-done) | copy-start | bytes 14155780
  221.3 3.0 copy-start.13
  224.3 1.3 copy-start.29
  229.8 1.1 copy-start.7
  239.4 1.1 copy-start.7
  249.0 1.1 copy-start.7
  261.0 1.4 copy-start.1
  261.0 0.9 copy-start.15
  264.4 54.6 %reduce-scatter.8.cloned.1.call-start = ((), (), s32[]{:S(2)}) async-start(), calls=%async_computation.14 | async-start | bytes 1474560 | tf_op jit(solution)/shard_map/reduce_scatter | solution.py:299
  264.5 0.9 copy-start.17
  267.4 79.6 %reduce-scatter.14.cloned.1.call-start = ((), (), s32[]{:S(2)}) async-start(), calls=%async_computation.17 | async-start | bytes 1474560 | tf_op jit(solution)/shard_map/reduce_scatter | solution.py:308
  270.4 105.4 %reduce-scatter.12.cloned.1.call-start = ((), (), s32[]{:S(2)}) async-start(), calls=%async_computation.16 | async-start | bytes 1474560 | tf_op jit(solution)/shard_map/reduce_scatter | solution.py:305
  270.5 3.3 copy-start.3
  273.8 152.4 %reduce-scatter.16.cloned.1.call-start = ((), (), s32[]{:S(2)}) async-start(), calls=%async_computation.18 | async-start | bytes 5898240 | tf_op jit(solution)/shard_map/reduce_scatter | solution.py:197
  280.1 196.6 %reduce-scatter.18.cloned.1.call-start = ((), (), s32[]{:S(2)}) async-start(), calls=%async_computation.19 | async-start | bytes 5898240 | tf_op jit(solution)/shard_map/reduce_scatter | solution.py:200
  286.5 1.1 copy-start.14
  286.5 240.6 %reduce-scatter.20.cloned.1.call-start = ((), (), s32[]{:S(2)}) async-start(), calls=%async_computation.20 | async-start | bytes 5898240 | tf_op jit(solution)/shard_map/reduce_scatter | solution.py:203
  294.4 407.3 %all-reduce.10.cloned.1.call-start = ((), (), s32[]{:S(2)}) async-start(), calls=%async_computation.21 | async-start | bytes 9437184 | tf_op jit(solution)/shard_map/psum | solution.py:314
  527.1 1.1 copy-start.16
  528.2 2.2 copy-start.18
  528.2 2.3 copy-start.28
  530.5 1.3 copy-start.9
  531.8 33.5 %copy-start.23 = (f32[512]{0:T(512)S(1)}, f32[512]{0:T(512)}, u32[]{:S(2)}) copy-start(f32[512]{0:T(512)} %get-tuple-element.222) | copy-start | bytes 6148
  565.2 3.1 copy-start.6
  565.2 3.1 copy-start.34
  701.8 3.0 copy-start.11
  704.8 1.7 copy-start.10
  706.5 1.6 copy-start.22
  706.5 2.4 copy-start.21
  708.1 1.7 copy-start.20
  708.1 2.6 copy-start.19
Sparse Core Ops, SparseCore 0:
  9.5 20.1 all-gather.7
  31.3 17.5 all-gather.9
  50.4 17.4 all-gather.11
  69.3 17.4 all-gather.13
  88.2 37.4 all-gather.15
  127.1 37.4 all-gather.17
  166.1 37.4 all-gather.19
  264.5 25.6 reduce-scatter.9
  293.3 25.6 reduce-scatter.7
  321.4 25.6 reduce-scatter.13
  350.2 25.6 reduce-scatter.11
  378.2 47.9 reduce-scatter.15
  428.7 47.9 reduce-scatter.17
  479.1 47.9 reduce-scatter.19
  531.5 170.2 all-reduce.9
where the time goes:
time: 728 us; the launch traced here: 718 us
  waiting for transfers between devices  499 us (69%)
  matrix products  122 us (17%)
  blocking collectives  37.4 us (5%)
  other arithmetic  28.5 us (4%)
  between operations  15.9 us (2%)
  local copies, waits for them, and re-layouts  13.8 us (2%)
    psum x1, waiting for transfers between devices, per_device(): lax.psum(attn_shares[1].astype(jnp.bfloat16), 'replica').astype(jnp.float32)  128 us
    reduce_scatter x1, waiting for transfers between devices, per_device(): lax.psum_scatter(ffn_terms[2].astype(jnp.bfloat16), 'shard', scatter_dime...  50.5 us
    reduce_scatter x1, waiting for transfers between devices, per_device(): lax.psum_scatter(ffn_terms[1].astype(jnp.bfloat16), 'shard', scatter_dime...  50.4 us
    reduce_scatter x1, waiting for transfers between devices, per_device(): lax.psum_scatter(ffn_terms[3].astype(jnp.bfloat16), 'shard', scatter_dime...  50.4 us
    all_gather x1, waiting for transfers between devices, per_device(): lax.all_gather(gate_weight, 'shard', axis=0, tiled=True)  35.1 us
    all_gather x1, waiting for transfers between devices, per_device(): lax.all_gather(down_weight, 'shard', axis=0, tiled=True)  32.2 us
    all_gather x1, waiting for transfers between devices, per_device(): lax.all_gather(up_weight, 'shard', axis=0, tiled=True)  32.1 us
    reduce_scatter x1, waiting for transfers between devices, per_device(): lax.psum_scatter(attn_terms[3].astype(jnp.bfloat16), 'shard', scatter_dim...  28.8 us
  transfers between devices with their start and end apart: 15, of which 14 were waited for; matrix products, arithmetic and copies ran while one was open for 13% of the time, Pallas kernels for 0%

commit v1 on v0

--- a/solution.py
+++ b/solution.py
@@ -309,9 +309,10 @@
             attn_terms[4].astype(jnp.bfloat16), "shard", scatter_dimension=0, tiled=True
         ).astype(jnp.float32),
     )
+    _follow_tables = lambda q_in: jnp.sum(lax.all_gather(q_in, "replica"), 0)
     attn_sums = (
         lax.psum(attn_shares[0].astype(jnp.bfloat16), "replica").astype(jnp.float32),
-        lax.psum(attn_shares[1].astype(jnp.bfloat16), "replica").astype(jnp.float32),
+        _follow_tables(attn_shares[1].astype(jnp.bfloat16)).astype(jnp.float32),
         lax.psum(attn_shares[2].astype(jnp.bfloat16), "replica").astype(jnp.float32),
         lax.psum(attn_shares[3].astype(jnp.bfloat16), "replica").astype(jnp.float32),
         lax.psum(attn_shares[4].astype(jnp.bfloat16), "replica").astype(jnp.float32),

time: 728 us -> 771 us (1.059)
  waiting for transfers between devices: 499 us -> 542 us
    psum x1, waiting for transfers between devices: 128 us -> 162 us  [per_device(): lax.psum(attn_shares[2].astype(jnp.bfloat16), 'replica').astype(jnp.float32)]
    reduce_scatter x1, waiting for transfers between devices: 24.4 us -> 0.02 us  [per_device(): lax.psum_scatter(attn_terms[1].astype(jnp.bfloat16), 'shard', scatter_dim...]
    reduce_scatter x1, waiting for transfers between devices: 0.02 us -> 23.9 us  [per_device(): lax.psum_scatter(attn_terms[2].astype(jnp.bfloat16), 'shard', scatter_dim...]
    all_gather x0 -> x1, waiting for transfers between devices: none -> 8.03 us  [per_device(): _follow_tables = lambda q_in: jnp.sum(lax.all_gather(q_in, 'replica'), 0)]
  transfers between devices with their start and end apart: 15 -> 16, of which waited for: 14 -> 15; matrix products, arithmetic and copies ran while one was open for 13% -> 12% of each run, Pallas kernels for 0% -> 0%
where the time goes in v1:
time: 771 us; the launch traced here: 762 us
  waiting for transfers between devices  542 us (70%)
  matrix products  122 us (16%)
  blocking collectives  36.2 us (5%)
  other arithmetic  30.6 us (4%)
  between operations  16 us (2%)
  local copies, waits for them, and re-layouts  13.8 us (2%)
    psum x1, waiting for transfers between devices, per_device(): lax.psum(attn_shares[2].astype(jnp.bfloat16), 'replica').astype(jnp.float32)  162 us
    reduce_scatter x1, waiting for transfers between devices, per_device(): lax.psum_scatter(ffn_terms[2].astype(jnp.bfloat16), 'shard', scatter_dime...  50.5 us
    reduce_scatter x1, waiting for transfers between devices, per_device(): lax.psum_scatter(ffn_terms[1].astype(jnp.bfloat16), 'shard', scatter_dime...  50.4 us
    reduce_scatter x1, waiting for transfers between devices, per_device(): lax.psum_scatter(ffn_terms[3].astype(jnp.bfloat16), 'shard', scatter_dime...  50.4 us
    all_gather x1, waiting for transfers between devices, per_device(): lax.all_gather(gate_weight, 'shard', axis=0, tiled=True)  35.1 us
    all_gather x1, waiting for transfers between devices, per_device(): lax.all_gather(down_weight, 'shard', axis=0, tiled=True)  32.2 us
    all_gather x1, waiting for transfers between devices, per_device(): lax.all_gather(up_weight, 'shard', axis=0, tiled=True)  32.1 us
    reduce_scatter x1, waiting for transfers between devices, per_device(): lax.psum_scatter(attn_terms[3].astype(jnp.bfloat16), 'shard', scatter_dim...  28.8 us
  transfers between devices with their start and end apart: 16, of which 15 were waited for; matrix products, arithmetic and copies ran while one was open for 12% of the time, Pallas kernels for 0%

profile of v1, /device:TPU:0, one launch (start us, length us, event | category | flops | bytes accessed | tf_op | source)
XLA Modules:
  0.0 761.8 jit_solution(1210851081440912295)
XLA Ops:
  15.5 8.7 %all-reduce.7 = (bf16[768]{0:T(1024)(128)(2,1)S(1)}, bf16[768]{0:T(1024)(128)(2,1)S(1)}) all-reduce(bf16[768]{0:T(1024)(128)(2,1)S(1)} %dynamic-update-slice, bf16[768]{0:T(1024)(128)(2,1)S(1)} %dynamic-update-slice.1), channel_id=1, replica_groups=mesh['shard'=4,'replica'=8] {'shard'}, use_global_device_ids=true, to_apply=%add | all-reduce | flops 1536 | bytes 6144
  25.1 2.1 copy.79
  28.2 1.6 all-gather.10.cloned.1.call-done
  29.8 2.1 convolution_convert_fusion.8
  33.0 15.8 %all-gather.12.cloned.1.call-done = bf16[768,768]{1,0:T(8,128)(2,1)} async-done(((bf16[192,768]{1,0:T(8,128)(2,1)}), bf16[768,768]{1,0:T(8,128)(2,1)}) %all-gather.12.cloned.1.call-update) | async-done | bytes 1179664 | tf_op jit(solution)/shard_map/all_gather | solution.py:112
  48.9 2.2 fusion.82
  51.1 16.9 %all-gather.14.cloned.1.call-done = bf16[768,768]{1,0:T(8,128)(2,1)} async-done(((bf16[192,768]{1,0:T(8,128)(2,1)}), bf16[768,768]{1,0:T(8,128)(2,1)}) %all-gather.14.cloned.1.call-update) | async-done | bytes 1179664 | tf_op jit(solution)/shard_map/all_gather | solution.py:113
  67.9 2.2 fusion.80
  70.8 15.3 %while.30 = (s32[]{:T(128)}, bf16[3,512,4,64]{1,3,2,0:T(8,128)(2,1)}, f32[3,4,512]{2,1,0:T(4,128)S(1)}, bf16[3,512,4,64]{1,3,2,0:T(8,128)(2,1)}, bf16[3,512,4,64...) while((s32[]{:T(128)}, ...), condition=%wide.region_6.7_spmd.clone.clone, body=%wide.region_3.6_spmd.clone.sunk.clone | while | flops 281802752 | bytes 15011921 | solution.py:145
  72.8 3.0 fusion.166
  77.9 3.0 fusion.166
  83.0 3.0 fusion.166
  86.8 2.4 multiply_reduce_fusion.3
  90.6 35.1 %all-gather.18.cloned.1.call-done = bf16[768,3072]{1,0:T(8,128)(2,1)} async-done(((bf16[192,3072]{1,0:T(8,128)(2,1)}), bf16[768,3072]{1,0:T(8,128)(2,1)}) %all-gather.18.cloned.1.call-update) | async-done | bytes 4718608 | tf_op jit(solution)/shard_map/all_gather | solution.py:150
  125.7 6.8 fusion.87
  132.5 32.1 %all-gather.20.cloned.1.call-done = bf16[768,3072]{1,0:T(8,128)(2,1)} async-done(((bf16[192,3072]{1,0:T(8,128)(2,1)}), bf16[768,3072]{1,0:T(8,128)(2,1)}) %all-gather.20.cloned.1.call-update) | async-done | bytes 4718608 | tf_op jit(solution)/shard_map/all_gather | solution.py:151
  164.6 6.8 fusion.88
  171.4 32.2 %all-gather.22.cloned.1.call-done = bf16[3072,768]{1,0:T(8,128)(2,1)} async-done(((bf16[768,768]{1,0:T(8,128)(2,1)}), bf16[3072,768]{1,0:T(8,128)(2,1)}) %all-gather.22.cloned.1.call-update) | async-done | bytes 4718608 | tf_op jit(solution)/shard_map/all_gather | solution.py:152
  203.6 10.4 %multiply_convert_fusion.1 = (bf16[512,3072]{1,0:T(8,128)(2,1)S(1)}, bf16[512,3072]{1,0:T(8,128)(2,1)S(1)}, bf16[512,3072]{1,0:T(8,128)(2,1)}) fusion(f32[512,3072]{1,0:T(8,128)} %fusion.87, f32[512,3072]{1,0:T(8,128)} %fusion.88, bf16[3072,768]{1,0:T(8,128)(2,1)} %all-gather.22.cloned.1.call-done, bf16[512,768]{1,0:T(8,128)(2,1)S(1)} %copy-done.12, ...), kind=kOutput, calls=%fused_computation.64 | convolution fusion | flops 2440691712 | bytes 27527168 | tf_op jit(solution)/shard_map/nd,fd->nf/dot_general | solution.py:172
  214.0 7.3 fusion.89
  221.4 3.0 multiply_reduce_fusion.1
  225.6 1.7 convolution_convert_fusion.7
  227.3 2.3 copy.64
  229.7 28.9 %while.31 = (s32[]{:T(128)}, f32[3,512,4,64]{1,3,2,0:T(8,128)}, f32[3,512,4,64]{1,3,2,0:T(8,128)}, bf16[3,512,4,64]{1,3,2,0:T(8,128)(2,1)}, bf16[3,512,4,64]{1,3...) while((s32[]{:T(128)}, f32[3,512,4,64]{1,3,2,0:T(8,128)}, ...), condition=%wide.region_11.12_spmd.clone.clone, body=%wide.region_9.11_spmd.clone.sunk.clone | while | flops 687863808 | bytes 39124100 | solution.py:256
  231.0 2.5 multiply_reduce_fusion.6
  233.4 1.3 multiply_convert_fusion.8
  234.7 1.6 fusion.178
  236.2 1.3 fusion.177
  237.5 1.9 fusion.179
  240.6 2.4 multiply_reduce_fusion.6
  243.0 1.3 multiply_convert_fusion.8
  244.3 1.6 fusion.178
  247.1 1.9 fusion.179
  250.1 2.5 multiply_reduce_fusion.6
  252.6 1.3 multiply_convert_fusion.8
  253.9 1.6 fusion.178
  255.4 1.3 fusion.177
  256.7 1.9 fusion.179
  258.6 2.4 add_convert_fusion
  262.4 2.0 convolution_convert_fusion.6
  265.4 2.0 convolution_convert_fusion.5
  267.5 2.9 convolution_convert_fusion.3
  270.5 3.3 convolution_convert_fusion.4
  273.8 6.2 convolution_convert_fusion.2
  280.1 6.3 convolution_convert_fusion.1
  287.6 6.8 convolution_convert_fusion
  295.1 23.9 %reduce-scatter.10.cloned.1.call-done = bf16[192,768]{1,0:T(8,128)(2,1)} async-done(((bf16[768,768]{1,0:T(8,128)(2,1)}), bf16[192,768]{1,0:T(8,128)(2,1)}) %reduce-scatter.10.cloned.1.call-update) | async-done | bytes 294928 | tf_op jit(solution)/shard_map/reduce_scatter | solution.py:302
  319.0 28.1 %reduce-scatter.14.cloned.1.call-done = bf16[192,768]{1,0:T(8,128)(2,1)} async-done(((bf16[768,768]{1,0:T(8,128)(2,1)}), bf16[192,768]{1,0:T(8,128)(2,1)}) %reduce-scatter.14.cloned.1.call-update) | async-done | bytes 294928 | tf_op jit(solution)/shard_map/reduce_scatter | solution.py:308
  347.0 28.8 %reduce-scatter.12.cloned.1.call-done = bf16[192,768]{1,0:T(8,128)(2,1)} async-done(((bf16[768,768]{1,0:T(8,128)(2,1)}), bf16[192,768]{1,0:T(8,128)(2,1)}) %reduce-scatter.12.cloned.1.call-update) | async-done | bytes 294928 | tf_op jit(solution)/shard_map/reduce_scatter | solution.py:305
  375.8 50.4 %reduce-scatter.16.cloned.1.call-done = bf16[192,3072]{1,0:T(8,128)(2,1)} async-done(((bf16[768,3072]{1,0:T(8,128)(2,1)}), bf16[192,3072]{1,0:T(8,128)(2,1)}) %reduce-scatter.16.cloned.1.call-update) | async-done | bytes 1179664 | tf_op jit(solution)/shard_map/reduce_scatter | solution.py:197
  426.2 50.5 %reduce-scatter.18.cloned.1.call-done = bf16[192,3072]{1,0:T(8,128)(2,1)} async-done(((bf16[768,3072]{1,0:T(8,128)(2,1)}), bf16[192,3072]{1,0:T(8,128)(2,1)}) %reduce-scatter.18.cloned.1.call-update) | async-done | bytes 1179664 | tf_op jit(solution)/shard_map/reduce_scatter | solution.py:200
  476.8 50.4 %reduce-scatter.20.cloned.1.call-done = bf16[768,768]{1,0:T(8,128)(2,1)} async-done(((bf16[3072,768]{1,0:T(8,128)(2,1)}), bf16[768,768]{1,0:T(8,128)(2,1)}) %reduce-scatter.20.cloned.1.call-update) | async-done | bytes 1179664 | tf_op jit(solution)/shard_map/reduce_scatter | solution.py:203
  528.3 2.2 fusion.91
  531.8 3.5 fusion.68
  535.3 5.7 all-reduce.6
  541.2 21.8 %all-reduce.4 = (bf16[192]{0:T(256)(128)(2,1)S(1)}, bf16[192]{0:T(256)(128)(2,1)S(1)}) all-reduce(bf16[192]{0:T(256)(128)(2,1)S(1)} %dynamic-slice.3, bf16[192]{0:T(256)(128)(2,1)S(1)} %dynamic-slice.5), channel_id=1, replica_groups=mesh['shard'=4,'replica'=8] {'replica'}, use_global_device_ids=true, to_apply=%region_15.16 | all-reduce | flops 384 | bytes 1536 | tf_op jit(solution)/shard_map/psum | solution.py:314
  564.1 3.1 fusion.65
  567.2 5.9 multiply_convert_fusion.4
  573.1 8.0 %all-gather.24.cloned.1.call-done = bf16[1536,768]{1,0:T(8,128)(2,1)} async-done(((bf16[192,768]{1,0:T(8,128)(2,1)}), bf16[1536,768]{1,0:T(8,128)(2,1)}) %all-gather.24.cloned.1.call-update) | async-done | bytes 2359312 | tf_op jit(solution)/shard_map/all_gather | solution.py:312
  581.1 2.1 reduce_sum.99
  584.1 162.2 %all-reduce.10.cloned.1.call-done = (bf16[192,768]{1,0:T(8,128)(2,1)}, bf16[192,768]{1,0:T(8,128)(2,1)}, bf16[192,768]{1,0:T(8,128)(2,1)}, bf16[192,3072]{1,0:T(...) async-done(((bf16[192,768]{1,0:T(8,128)(2,1)}, bf16[192,768]{1,0:T(8,128)(2,1)}, bf16[192,768]{1,0:T(8,128)(2,1)}, bf16[192,3072]{1,0:T(8,128)(2,1)}, ...) | async-done | bytes 4423696 | tf_op jit(solution)/shard_map/psum | solution.py:316
  746.2 3.0 convert_element_type.216
  749.2 1.7 convert_element_type.218
  750.9 1.6 convert_element_type.220
  (170 shorter events, 36.0 us)
Async XLA Ops:
  7.2 22.6 %all-gather.10.cloned.1.call-start = ((), (), s32[]{:S(2)}) async-start(), calls=%async_computation.7 | async-start | bytes 1474560 | tf_op jit(solution)/shard_map/all_gather | solution.py:114
  7.9 41.0 %all-gather.12.cloned.1.call-start = ((), (), s32[]{:S(2)}) async-start(), calls=%async_computation.8 | async-start | bytes 1474560 | tf_op jit(solution)/shard_map/all_gather | solution.py:112
  8.7 59.3 %all-gather.14.cloned.1.call-start = ((), (), s32[]{:S(2)}) async-start(), calls=%async_computation.9 | async-start | bytes 1474560 | tf_op jit(solution)/shard_map/all_gather | solution.py:113
  9.4 77.4 %all-gather.16.cloned.1.call-start = ((), (), s32[]{:S(2)}) async-start(), calls=%async_computation.10 | async-start | bytes 1474560 | tf_op jit(solution)/shard_map/all_gather | solution.py:115
  10.0 115.7 %all-gather.18.cloned.1.call-start = ((), (), s32[]{:S(2)}) async-start(), calls=%async_computation.11 | async-start | bytes 5898240 | tf_op jit(solution)/shard_map/all_gather | solution.py:150
  10.6 2.4 copy-start.25
  10.6 2.4 copy-start.26
  10.6 3.2 copy-start.23
  10.6 4.4 copy-start.29
  10.6 4.7 copy-start.30
  10.6 13.6 %copy-start = (bf16[512,768]{1,0:T(8,128)(2,1)S(1)}, bf16[512,768]{1,0:T(8,128)(2,1)}, u32[]{:S(2)}) copy-start(bf16[512,768]{1,0:T(8,128)(2,1)} %param.18) | copy-start | bytes 2359300
  10.6 153.9 %all-gather.20.cloned.1.call-start = ((), (), s32[]{:S(2)}) async-start(), calls=%async_computation.12 | async-start | bytes 5898240 | tf_op jit(solution)/shard_map/all_gather | solution.py:151
  11.2 13.8 %copy-start.24 = (s32[512]{0:T(512)S(1)}, s32[512]{0:T(512)}, u32[]{:S(2)}) copy-start(s32[512]{0:T(512)} %param.22) | copy-start | bytes 6148
  11.2 192.4 %all-gather.22.cloned.1.call-start = ((), (), s32[]{:S(2)}) async-start(), calls=%async_computation.13 | async-start | bytes 5898240 | tf_op jit(solution)/shard_map/all_gather | solution.py:152
  12.0 282.6 %reduce-scatter.8.cloned.1.call-start = ((), (), s32[]{:S(2)}) async-start(), calls=%async_computation.14 | async-start | bytes 1474560 | tf_op jit(solution)/shard_map/reduce_scatter | solution.py:299
  89.2 1.1 copy-start.4
  90.6 74.0 %copy-start.2 = (bf16[512,768]{1,0:T(8,128)(2,1)}, bf16[512,768]{1,0:T(8,128)(2,1)S(1)}, u32[]{:S(2)}) copy-start(bf16[512,768]{1,0:T(8,128)(2,1)S(1)} %multiply_convert_fusion.5) | copy-start | bytes 2359300
  132.5 71.1 %copy-start.12 = (bf16[512,768]{1,0:T(8,128)(2,1)S(1)}, bf16[512,768]{1,0:T(8,128)(2,1)}, u32[]{:S(2)}) copy-start(bf16[512,768]{1,0:T(8,128)(2,1)} %param.19) | copy-start | bytes 2359300
  214.0 7.3 copy-start.32
  214.0 7.3 copy-start.31
  214.0 7.3 copy-start.5
  214.0 7.3 copy-start.8
  221.4 3.0 copy-start.13
  224.3 1.3 copy-start.28
  229.8 1.1 copy-start.7
  239.4 1.1 copy-start.7
  249.0 1.1 copy-start.7
  261.0 1.4 copy-start.1
  261.0 0.9 copy-start.15
  264.4 54.6 %reduce-scatter.10.cloned.1.call-start = ((), (), s32[]{:S(2)}) async-start(), calls=%async_computation.15 | async-start | bytes 1474560 | tf_op jit(solution)/shard_map/reduce_scatter | solution.py:302
  264.5 0.9 copy-start.17
  267.4 79.6 %reduce-scatter.14.cloned.1.call-start = ((), (), s32[]{:S(2)}) async-start(), calls=%async_computation.17 | async-start | bytes 1474560 | tf_op jit(solution)/shard_map/reduce_scatter | solution.py:308
  270.5 105.4 %reduce-scatter.12.cloned.1.call-start = ((), (), s32[]{:S(2)}) async-start(), calls=%async_computation.16 | async-start | bytes 1474560 | tf_op jit(solution)/shard_map/reduce_scatter | solution.py:305
  270.5 3.3 copy-start.3
  273.8 152.4 %reduce-scatter.16.cloned.1.call-start = ((), (), s32[]{:S(2)}) async-start(), calls=%async_computation.18 | async-start | bytes 5898240 | tf_op jit(solution)/shard_map/reduce_scatter | solution.py:197
  280.1 196.7 %reduce-scatter.18.cloned.1.call-start = ((), (), s32[]{:S(2)}) async-start(), calls=%async_computation.19 | async-start | bytes 5898240 | tf_op jit(solution)/shard_map/reduce_scatter | solution.py:200
  286.5 1.1 copy-start.14
  286.5 240.7 %reduce-scatter.20.cloned.1.call-start = ((), (), s32[]{:S(2)}) async-start(), calls=%async_computation.20 | async-start | bytes 5898240 | tf_op jit(solution)/shard_map/reduce_scatter | solution.py:203
  294.5 286.7 %all-gather.24.cloned.1.call-start = ((), (), s32[]{:S(2)}) async-start(), calls=%async_computation.21 | async-start | bytes 2654208 | tf_op jit(solution)/shard_map/all_gather | solution.py:312
  295.1 451.2 %all-reduce.10.cloned.1.call-start = ((), (), s32[]{:S(2)}) async-start(), calls=%async_computation.22 | async-start | bytes 8847360 | tf_op jit(solution)/shard_map/psum | solution.py:316
  527.2 1.1 copy-start.18
  528.3 2.2 copy-start.16
  528.3 2.3 copy-start.27
  530.6 1.3 copy-start.9
  531.8 32.2 %copy-start.22 = (f32[512]{0:T(512)S(1)}, f32[512]{0:T(512)}, u32[]{:S(2)}) copy-start(f32[512]{0:T(512)} %get-tuple-element.221) | copy-start | bytes 6148
  564.1 3.1 copy-start.6
  564.1 3.1 copy-start.33
  746.2 3.0 copy-start.11
  749.2 1.7 copy-start.10
  750.9 1.6 copy-start.21
  750.9 2.4 copy-start.20
  752.5 1.7 copy-start.19
Sparse Core Ops, SparseCore 0:
  9.5 20.1 all-gather.9
  31.3 17.5 all-gather.11
  50.4 17.4 all-gather.13
  69.3 17.4 all-gather.15
  88.2 37.4 all-gather.17
  127.1 37.4 all-gather.19
  166.1 37.4 all-gather.21
  264.5 25.6 reduce-scatter.7
  293.3 25.6 reduce-scatter.9
  321.4 25.6 reduce-scatter.13
  350.2 25.6 reduce-scatter.11
  378.2 47.9 reduce-scatter.15
  428.8 47.9 reduce-scatter.17
  479.2 47.9 reduce-scatter.19
  529.2 51.8 all-gather.23
  585.4 160.7 all-reduce.9
